TPU v7x, 512 devices: a whole 4x8x8 slice. The times are simulated.
512 devices in a mesh: space: 64 (over y_lo, z, x), tensor: 8 (over y_hi, core).
Axes of the slice: x: 4, y: 8 (y_hi: 4, y_lo: 2; y = y_hi * 2 + y_lo), z: 8, core: 2. Of those that a mesh axis runs over, the one named last changes fastest.
Arguments:
- tokens: float32 [2, 128, 128, 2048], P(None, 'space', None, 'tensor'), may hold values from -6 to 6
- in_gain: float32 [2048], replicated, may hold values from 0.25 to 1.75
- w_inner: bfloat16 [2048, 3072], P(None, 'tensor'), may hold values from -0.125 to 0.125
- w_bc: bfloat16 [2048, 256], replicated, may hold values from -0.03125 to 0.03125
- w_step: bfloat16 [2048, 48], P(None, 'tensor'), may hold values from -0.125 to 0.125
- step_bias: float32 [48], P('tensor'), may hold values from -3 to 0
- decay_rate: float32 [48], P('tensor'), may hold values from 0.02 to 2
- skip: float32 [48], P('tensor'), may hold values from 0.5 to 2
- norm_gain: float32 [3072], P('tensor'), may hold values from 0.25 to 1.75
- w_out: bfloat16 [3072, 2048], P('tensor'), may hold values from -0.109375 to 0.109375
Outputs:
- mixed: bfloat16 [2, 128, 128, 2048], P(None, 'space', None, 'tensor')
All inputs are finite; a program needn't handle non-finite values.
Results may differ from a plain program's by a relative error of at most 0.011.
Values may be sent and summed in bfloat16 or wider, within the bound.
No kernel may reach another device: no remote copies, remote signals or barrier semaphores. Data moves between devices by JAX's collectives and lax.ppermute only.
A program may use at most 64 MiB of HBM per device.

v0:
```python
import jax
import jax.numpy as jnp
from jax import lax
from jax.sharding import PartitionSpec as P

HEAD_DIM = 64
STATE = 128
NORM_HEADS = 6
EPS = 1e-05


def kernel(logdecay):
    running = jnp.cumsum(logdecay, axis=-1)
    length = logdecay.shape[-1]
    place = jnp.arange(length)
    lower = place[:, None] >= place[None, :]
    upper = place[:, None] <= place[None, :]
    later = running[..., :, None] - running[..., None, :]
    shifted = running - logdecay
    earlier = shifted[..., None, :] - shifted[..., :, None]
    forward = jnp.exp(jnp.where(lower, later, -jnp.inf))
    backward = jnp.exp(jnp.where(upper, earlier, -jnp.inf))
    return forward + backward


def scan_grid(values, maps, logdecay, along_rows):
    heads = logdecay.shape[-1]
    in_map = maps[..., :STATE]
    out_map = maps[..., STATE:]
    split_values = values.reshape(values.shape[:3] + (heads, HEAD_DIM))
    if along_rows:
        scores = jnp.einsum("ialn,iamn->ialm", out_map, in_map, preferred_element_type=jnp.float32)
        decays = jnp.moveaxis(logdecay.astype(jnp.float32), 3, 2)
    else:
        scores = jnp.einsum("ilan,iman->ialm", out_map, in_map, preferred_element_type=jnp.float32)
        decays = jnp.transpose(logdecay.astype(jnp.float32), (0, 2, 3, 1))
    weights = (scores[:, :, None] * kernel(decays)).astype(jnp.bfloat16)
    if along_rows:
        result = jnp.einsum(
            "iahlm,iamhp->ialhp", weights, split_values, preferred_element_type=jnp.float32
        )
    else:
        result = jnp.einsum(
            "iahlm,imahp->ilahp", weights, split_values, preferred_element_type=jnp.float32
        )
    return result.reshape(values.shape)


def on_device(
    tokens, in_gain, w_inner, w_bc, w_step, step_bias, decay_rate, skip, norm_gain, w_out
):
    whole = lax.all_gather(tokens.astype(jnp.bfloat16), "tensor", axis=3, tiled=True)
    rounded = whole.astype(jnp.float32)
    scale = lax.rsqrt(jnp.mean(rounded * rounded, axis=-1, keepdims=True) + EPS)
    normed = (rounded * scale * in_gain).astype(jnp.bfloat16)
    inner = jnp.einsum("irwd,dc->irwc", normed, w_inner, preferred_element_type=jnp.float32).astype(
        jnp.bfloat16
    )
    maps = jnp.einsum("irwd,dc->irwc", normed, w_bc, preferred_element_type=jnp.float32).astype(
        jnp.bfloat16
    )
    step = jax.nn.softplus(
        jnp.einsum("irwd,dc->irwc", normed, w_step, preferred_element_type=jnp.float32) + step_bias
    )
    logdecay = (-decay_rate * step).astype(jnp.bfloat16)
    heads_local = w_step.shape[1]
    lead = inner.shape[:3]
    value = (
        (inner.reshape(lead + (heads_local, HEAD_DIM)).astype(jnp.float32) * step[..., None])
        .reshape(inner.shape)
        .astype(jnp.bfloat16)
    )
    col_value = lax.all_to_all(value, "space", split_axis=2, concat_axis=1, tiled=True)
    col_maps = lax.all_to_all(maps, "space", split_axis=2, concat_axis=1, tiled=True)
    col_decay = lax.all_to_all(logdecay, "space", split_axis=2, concat_axis=1, tiled=True)
    column_out = scan_grid(col_value, col_maps, col_decay, False).astype(jnp.bfloat16)
    column_back = lax.all_to_all(column_out, "space", split_axis=1, concat_axis=2, tiled=True)
    row_out = scan_grid(value, maps, logdecay, True)
    skip_wide = jnp.repeat(skip, HEAD_DIM)
    total = row_out + column_back.astype(jnp.float32) + skip_wide * inner.astype(jnp.float32)
    group = NORM_HEADS * HEAD_DIM
    grouped = total.reshape(lead + (inner.shape[3] // group, group))
    norm_scale = lax.rsqrt(jnp.mean(grouped * grouped, axis=-1, keepdims=True) + EPS)
    gated = ((grouped * norm_scale).reshape(inner.shape) * norm_gain).astype(jnp.bfloat16)
    partial_out = jnp.einsum("irwc,cd->irwd", gated, w_out, preferred_element_type=jnp.float32)
    mixer = lax.psum_scatter(partial_out, "tensor", scatter_dimension=3, tiled=True)
    return (tokens + mixer).astype(jnp.bfloat16)


def solution(mesh):
    return jax.shard_map(
        on_device,
        mesh=mesh,
        in_specs=(
            P(None, "space", None, "tensor"),
            P(),
            P(None, "tensor"),
            P(),
            P(None, "tensor"),
            P("tensor"),
            P("tensor"),
            P("tensor"),
            P("tensor"),
            P("tensor", None),
        ),
        out_specs=P(None, "space", None, "tensor"),
        check_vma=False,
    )
```

profile of v0, /device:TPU:19, one launch (start us, length us, event | category | flops | bytes accessed | tf_op | source)
XLA Modules:
  0.0 218.5 jit_solution(5063790395113188788)
XLA Ops:
  6.6 1.9 convert_element_type.76
  8.5 0.7 neg.11
  9.2 45.6 %all-gather.2.cloned.1.call-done = bf16[2,2,128,2048]{3,2,1,0:T(8,128)(2,1)} async-done(((bf16[2,2,128,256]{3,2,1,0:T(8,128)(2,1)}), bf16[2,2,128,2048]{3,2,1,0:T(8,128)(2,1)}) %all-gather.2.cloned.1.call-update) | async-done | bytes 2097168 | tf_op jit(solution)/shard_map/all_gather | solution.py:52
  54.7 2.2 %fusion = f32[2,2,128]{2,1,0:T(2,128)S(1)} fusion(bf16[2,2,128,2048]{3,2,1,0:T(8,128)(2,1)} %all-gather.2.cloned.1.call-done), kind=kLoop, calls=%fused_computation.2 | loop fusion | flops 3145216 | bytes 2099200 | tf_op jit(solution)/shard_map/reduce_sum | solution.py:54
  57.0 0.8 multiply_convert_fusion.7
  57.8 0.8 copy.52
  58.6 12.8 %all-to-all-start.2 = ((bf16[2,2,128,6]{3,1,0,2:T(2,128)(2,1)}), bf16[2,2,128,6]{3,1,0,2:T(2,128)(2,1)S(1)}, u32[]{:S(2)}, u32[]{:S(2)}) async-start(bf16[2,2,128,6]{3,1,0,2:T(2,128)(2,1)} %copy.52), calls=%async_computation.2 | async-start | bytes 262144 | tf_op jit(solution)/shard_map/all_to_all | solution.py:75
  71.5 2.4 %convolution_convert_fusion.1 = bf16[2,2,128,256]{3,2,1,0:T(8,128)(2,1)S(1)} fusion(bf16[2,2,128,2048]{3,2,1,0:T(8,128)(2,1)} %all-gather.2.cloned.1.call-done, f32[2048]{0:T(1024)S(1)} %copy-done.13, f32[2,2,128]{2,1,0:T(2,128)S(1)} %add_rsqrt_fusion.1, bf16[2048,256]{1,0:T(8,128)(2,1)S(1)} %copy-done.11), kind=kOutput, calls=%fused_computation.14 | convolution fusion | flops 541196288 | bytes 3418112 | tf_op jit(solution)/shard_map/irwd,dc->irwc/dot_general | solution.py:59
  73.8 1.0 copy.48
  74.8 5.6 %all-to-all-done.2 = bf16[2,2,128,6]{3,1,0,2:T(2,128)(2,1)S(1)} async-done(((bf16[2,2,128,6]{3,1,0,2:T(2,128)(2,1)}), bf16[2,2,128,6]{3,1,0,2:T(2,128)(2,1)S(1)}, u32[]{:S(2)}, u32[]{:S(2)}) %all-to-all-start.2) | async-done | bytes 6176 | tf_op jit(solution)/shard_map/all_to_all | solution.py:75
  80.5 6.1 %all-to-all-start.1 = ((bf16[2,2,128,256]{3,1,0,2:T(2,128)(2,1)}), bf16[2,2,128,256]{3,1,0,2:T(2,128)(2,1)S(1)}, u32[]{:S(2)}, u32[]{:S(2)}) async-start(bf16[2,2,128,256]{3,1,0,2:T(2,128)(2,1)} %copy.48), calls=%async_computation.1 | async-start | bytes 524288 | tf_op jit(solution)/shard_map/all_to_all | solution.py:74
  86.6 0.7 mul.106
  87.4 1.2 copy.44
  88.5 4.4 %multiply_convert_fusion.5 = (bf16[2,2,128,384]{3,2,1,0:T(8,128)(2,1)S(1)}, f32[2,2,128,384]{3,2,1,0:T(8,128)}) fusion(f32[2,2,128,384]{3,2,1,0:T(8,128)} %copy.44, bf16[2048,384]{1,0:T(8,128)(2,1)} %param.12, bf16[2,2,128,2048]{3,2,1,0:T(8,128)(2,1)} %all-gather.2.cloned.1.call-done, f32[2048]{0:T(1024)S(1)} %copy-done.13, ...), kind=kOutput, calls=%fused_computation.34 | convolution fusion | flops 810287104 | bytes 5646336 | tf_op jit(solution)/shard_map/irwd,dc->irwc/dot_general | solution.py:56
  92.9 1.1 copy.46
  94.1 2.0 all-to-all-done.1
  96.1 8.8 %all-to-all-start = ((bf16[2,2,128,384]{3,1,0,2:T(2,128)(2,1)}), bf16[2,2,128,384]{3,1,0,2:T(2,128)(2,1)S(1)}, u32[]{:S(2)}, u32[]{:S(2)}) async-start(bf16[2,2,128,384]{3,1,0,2:T(2,128)(2,1)} %copy.46), calls=%async_computation | async-start | bytes 786432 | tf_op jit(solution)/shard_map/all_to_all | solution.py:73
  106.1 1.1 reduce_window_sum.18
  108.4 6.6 %all-to-all-done = bf16[2,2,128,384]{3,1,0,2:T(2,128)(2,1)S(1)} async-done(((bf16[2,2,128,384]{3,1,0,2:T(2,128)(2,1)}), bf16[2,2,128,384]{3,1,0,2:T(2,128)(2,1)S(1)}, u32[]{:S(2)}, u32[]{:S(2)}) %all-to-all-start) | async-done | bytes 393248 | tf_op jit(solution)/shard_map/all_to_all | solution.py:73
  115.3 1.6 reshape.67
  116.9 2.5 %convolution_convert_fusion = bf16[2,2,6,64,128]{4,3,2,1,0:T(8,128)(2,1)S(1)} fusion(bf16[2,128,2,6,64]{4,3,2,1,0:T(8,128)(2,1)} %reshape.67, f32[2,2,6,128]{3,2,1,0:T(8,128)} %bitcast_subtract_fusion, f32[2,2,6,128]{3,2,1,0:T(8,128)} %copy-done.3, f32[2,2,128,128]{3,2,1,0:T(8,128)S(1)} %fusion.40, pred[128,128]{1,0:T(8,128)(4,1)} %get-tuple-element.14, ...), kind=kOutput, calls=%fused_computation.13 | convolution fusion | flops 53280768 | bytes 1105920 | tf_op jit(solution)/shard_map/iahlm,imahp->ilahp/dot_general | solution.py:43
  119.4 1.1 copy.58
  120.5 10.5 %all-to-all-start.3 = ((bf16[2,128,2,384]{3,2,0,1:T(2,128)(2,1)}), bf16[2,128,2,384]{3,2,0,1:T(2,128)(2,1)S(1)}, u32[]{:S(2)}, u32[]{:S(2)}) async-start(bf16[2,128,2,384]{3,2,0,1:T(2,128)(2,1)} %copy.58), calls=%async_computation.3 | async-start | bytes 786432 | tf_op jit(solution)/shard_map/all_to_all | solution.py:77
  131.6 1.2 reduce_window_sum.17
  133.0 2.0 fusion.17
  135.1 1.4 copy.62
  136.5 4.8 %all-to-all-done.3 = bf16[2,128,2,384]{3,2,0,1:T(2,128)(2,1)S(1)} async-done(((bf16[2,128,2,384]{3,2,0,1:T(2,128)(2,1)}), bf16[2,128,2,384]{3,2,0,1:T(2,128)(2,1)S(1)}, u32[]{:S(2)}, u32[]{:S(2)}) %all-to-all-start.3) | async-done | bytes 393248 | tf_op jit(solution)/shard_map/all_to_all | solution.py:77
  142.2 1.4 reshape.68
  143.7 1.6 multiply_reduce_fusion
  145.3 3.3 %fusion.3 = f32[2,2,128,2048]{3,2,1,0:T(8,128)} fusion(bf16[384,2048]{1,0:T(8,128)(2,1)S(1)} %copy-done, f32[2,2,128,384]{3,2,1,0:T(8,128)S(1)} %get-tuple-element.6, f32[384]{0:T(512)S(1)} %copy-done.7, f32[2,2,128]{2,1,0:T(2,128)S(1)} %add_rsqrt_fusion), kind=kOutput, calls=%fused_computation.5 | convolution fusion | flops 805896192 | bytes 6557184 | tf_op jit(solution)/shard_map/irwc,cd->irwd/dot_general | solution.py:85
  148.6 61.3 %reduce-scatter.2.cloned.1.call-done = f32[2,2,128,256]{3,2,1,0:T(8,128)} async-done(((f32[2,2,128,2048]{3,2,1,0:T(8,128)}), f32[2,2,128,256]{3,2,1,0:T(8,128)}) %reduce-scatter.2.cloned.1.call-update) | async-done | bytes 524304 | tf_op jit(solution)/shard_map/reduce_scatter | solution.py:86
  209.8 1.8 add_convert_fusion
  (55 shorter events, 4.7 us)
Async XLA Ops:
  6.5 138.7 %copy-start = (bf16[384,2048]{1,0:T(8,128)(2,1)S(1)}, bf16[384,2048]{1,0:T(8,128)(2,1)}, u32[]{:S(2)}) copy-start(bf16[384,2048]{1,0:T(8,128)(2,1)} %param.19) | copy-start | bytes 4718596
  6.5 50.4 %copy-start.13 = (f32[2048]{0:T(1024)S(1)}, f32[2048]{0:T(1024)}, u32[]{:S(2)}) copy-start(f32[2048]{0:T(1024)} %param.11) | copy-start | bytes 24580
  6.5 50.4 %copy-start.14 = (f32[6]{0:T(128)S(1)}, f32[6]{0:T(128)}, u32[]{:S(2)}) copy-start(f32[6]{0:T(128)} %param.15) | copy-start | bytes 76
  6.5 50.5 %copy-start.12 = (bf16[2048,6]{0,1:T(8,128)(2,1)S(1)}, bf16[2048,6]{0,1:T(8,128)(2,1)}, u32[]{:S(2)}) copy-start(bf16[2048,6]{0,1:T(8,128)(2,1)} %param.14) | copy-start | bytes 73732
  6.5 48.2 %all-gather.2.cloned.1.call-start = ((), (), s32[]{:S(2)}) async-start(), calls=%async_computation.5 | async-start | bytes 2359296 | tf_op jit(solution)/shard_map/all_gather | solution.py:52
  9.2 48.7 %copy-start.8 = (f32[6]{0:T(128)}, f32[6]{0:T(128)S(1)}, u32[]{:S(2)}) copy-start(f32[6]{0:T(128)S(1)} %neg.11) | copy-start | bytes 76
  54.7 2.3 %copy-start.1 = (bf16[2,2,128,2048]{3,2,1,0:T(8,128)(2,1)S(1)}, bf16[2,2,128,2048]{3,2,1,0:T(8,128)(2,1)}, u32[]{:S(2)}) copy-start(bf16[2,2,128,2048]{3,2,1,0:T(8,128)(2,1)} %all-gather.2.cloned.1.call-done) | copy-start | bytes 6291460
  57.0 14.4 %copy-start.11 = (bf16[2048,256]{1,0:T(8,128)(2,1)S(1)}, bf16[2048,256]{1,0:T(8,128)(2,1)}, u32[]{:S(2)}) copy-start(bf16[2048,256]{1,0:T(8,128)(2,1)} %param.13) | copy-start | bytes 3145732
  58.6 21.8 %all-to-all-start.2 = ((bf16[2,2,128,6]{3,1,0,2:T(2,128)(2,1)}), bf16[2,2,128,6]{3,1,0,2:T(2,128)(2,1)S(1)}, u32[]{:S(2)}, u32[]{:S(2)}) async-start(bf16[2,2,128,6]{3,1,0,2:T(2,128)(2,1)} %copy.52), calls=%async_computation.2 | async-start | bytes 262144 | tf_op jit(solution)/shard_map/all_to_all | solution.py:75
  71.5 15.1 %copy-start.10 = (f32[6]{0:T(128)S(1)}, f32[6]{0:T(128)}, u32[]{:S(2)}) copy-start(f32[6]{0:T(128)} %param.17) | copy-start | bytes 76
  80.5 15.6 %all-to-all-start.1 = ((bf16[2,2,128,256]{3,1,0,2:T(2,128)(2,1)}), bf16[2,2,128,256]{3,1,0,2:T(2,128)(2,1)S(1)}, u32[]{:S(2)}, u32[]{:S(2)}) async-start(bf16[2,2,128,256]{3,1,0,2:T(2,128)(2,1)} %copy.48), calls=%async_computation.1 | async-start | bytes 524288 | tf_op jit(solution)/shard_map/all_to_all | solution.py:74
  96.1 18.9 %all-to-all-start = ((bf16[2,2,128,384]{3,1,0,2:T(2,128)(2,1)}), bf16[2,2,128,384]{3,1,0,2:T(2,128)(2,1)S(1)}, u32[]{:S(2)}, u32[]{:S(2)}) async-start(bf16[2,2,128,384]{3,1,0,2:T(2,128)(2,1)} %copy.46), calls=%async_computation | async-start | bytes 786432 | tf_op jit(solution)/shard_map/all_to_all | solution.py:73
  107.2 7.8 %copy-start.3 = (f32[2,2,6,128]{3,2,1,0:T(8,128)}, f32[2,2,6,128]{3,2,1,0:T(8,128)S(1)}, u32[]{:S(2)}) copy-start(f32[2,2,6,128]{3,2,1,0:T(8,128)S(1)} %reduce_window_sum.18) | copy-start | bytes 36868
  119.4 11.9 %copy-start.9 = (f32[6]{0:T(128)S(1)}, f32[6]{0:T(128)}, u32[]{:S(2)}) copy-start(f32[6]{0:T(128)} %copy-done.8) | copy-start | bytes 76
  119.4 13.6 %copy-start.4 = (pred[128,128]{1,0:T(8,128)(4,1)S(1)}, pred[128,128]{1,0:T(8,128)(4,1)}, u32[]{:S(2)}) copy-start(pred[128,128]{1,0:T(8,128)(4,1)} %get-tuple-element.14) | copy-start | bytes 49156
  119.4 13.6 %copy-start.5 = (pred[128,128]{1,0:T(8,128)(4,1)S(1)}, pred[128,128]{1,0:T(8,128)(4,1)}, u32[]{:S(2)}) copy-start(pred[128,128]{1,0:T(8,128)(4,1)} %get-tuple-element.15) | copy-start | bytes 49156
  120.5 20.8 %all-to-all-start.3 = ((bf16[2,128,2,384]{3,2,0,1:T(2,128)(2,1)}), bf16[2,128,2,384]{3,2,0,1:T(2,128)(2,1)S(1)}, u32[]{:S(2)}, u32[]{:S(2)}) async-start(bf16[2,128,2,384]{3,2,0,1:T(2,128)(2,1)} %copy.58), calls=%async_computation.3 | async-start | bytes 786432 | tf_op jit(solution)/shard_map/all_to_all | solution.py:77
  131.0 78.8 %reduce-scatter.2.cloned.1.call-start = ((), (), s32[]{:S(2)}) async-start(), calls=%async_computation.6 | async-start | bytes 4718592 | tf_op jit(solution)/shard_map/reduce_scatter | solution.py:86
  141.9 1.7 copy-start.6
  143.7 1.6 copy-start.7
  148.6 61.3 %copy-start.2 = (f32[2,2,128,256]{3,2,1,0:T(8,128)S(1)}, f32[2,2,128,256]{3,2,1,0:T(8,128)}, u32[]{:S(2)}) copy-start(f32[2,2,128,256]{3,2,1,0:T(8,128)} %param.10) | copy-start | bytes 1572868
Sparse Core Ops, SparseCore 0:
  9.5 45.2 all-gather.1
  148.7 61.0 reduce-scatter.1
where the time goes:
time: 219 us; the launch traced here: 218 us
  waiting for transfers between devices  126 us (58%)
  starting transfers between devices  38.4 us (18%)
  matrix products  15.8 us (7%)
  between operations  13.7 us (6%)
  local copies, waits for them, and re-layouts  12.8 us (6%)
  other arithmetic  11.9 us (5%)
    reduce_scatter x1, waiting for transfers between devices, on_device(): lax.psum_scatter(partial_out, 'tensor', scatter_dimension=3, tiled=True)  61.3 us
    all_gather x1, waiting for transfers between devices, on_device(): lax.all_gather(tokens.astype(jnp.bfloat16), 'tensor', axis=3, tiled=True)  45.6 us
    all_to_all x1, starting transfers between devices, on_device(): lax.all_to_all(logdecay, 'space', split_axis=2, concat_axis=1, tiled=True)  12.8 us
    all_to_all x1, starting transfers between devices, on_device(): lax.all_to_all(column_out, 'space', split_axis=1, concat_axis=2, tiled=True)  10.5 us
    all_to_all x1, starting transfers between devices, on_device(): lax.all_to_all(value, 'space', split_axis=2, concat_axis=1, tiled=True)  8.77 us
    all_to_all x1, waiting for transfers between devices, on_device(): lax.all_to_all(value, 'space', split_axis=2, concat_axis=1, tiled=True)  6.57 us
    all_to_all x1, starting transfers between devices, on_device(): lax.all_to_all(maps, 'space', split_axis=2, concat_axis=1, tiled=True)  6.09 us
    all_to_all x1, waiting for transfers between devices, on_device(): lax.all_to_all(logdecay, 'space', split_axis=2, concat_axis=1, tiled=True)  5.64 us
  transfers between devices with their start and end apart: 6, of which 6 were waited for; matrix products, arithmetic and copies ran while one was open for 9% of the time, Pallas kernels for 0%

commit v1 on v0

--- a/solution.py
+++ b/solution.py
@@ -49,7 +49,7 @@
 def on_device(
     tokens, in_gain, w_inner, w_bc, w_step, step_bias, decay_rate, skip, norm_gain, w_out
 ):
-    whole = lax.all_gather(tokens.astype(jnp.bfloat16), "tensor", axis=3, tiled=True)
+    whole = jnp.concatenate(lax.all_gather(tokens.astype(jnp.bfloat16), "tensor"), axis=3)
     rounded = whole.astype(jnp.float32)
     scale = lax.rsqrt(jnp.mean(rounded * rounded, axis=-1, keepdims=True) + EPS)
     normed = (rounded * scale * in_gain).astype(jnp.bfloat16)

time: 219 us -> 217 us (level)
  starting transfers between devices: 38.4 us -> 36.1 us
    all_gather x1, waiting for transfers between devices: 45.6 us -> 43.3 us  [on_device(): lax.all_gather(tokens.astype(jnp.bfloat16), 'tensor')]
  transfers between devices with their start and end apart: 6 -> 6, of which waited for: 6 -> 6; matrix products, arithmetic and copies ran while one was open for 9% -> 8% of each run, Pallas kernels for 0% -> 0%
where the time goes in v1:
time: 217 us
  waiting for transfers between devices  125 us (58%)
  starting transfers between devices  36.1 us (17%)
  matrix products  15.4 us (7%)
  local copies, waits for them, and re-layouts  13.8 us (6%)
  between operations  13.7 us (6%)
  other arithmetic  12.2 us (6%)
    reduce_scatter x1, waiting for transfers between devices, on_device(): lax.psum_scatter(partial_out, 'tensor', scatter_dimension=3, tiled=True)  61.2 us
    all_gather x1, waiting for transfers between devices, on_device(): lax.all_gather(tokens.astype(jnp.bfloat16), 'tensor')  43.3 us
    all_to_all x1, starting transfers between devices, on_device(): lax.all_to_all(logdecay, 'space', split_axis=2, concat_axis=1, tiled=True)  10.9 us
    all_to_all x1, starting transfers between devices, on_device(): lax.all_to_all(column_out, 'space', split_axis=1, concat_axis=2, tiled=True)  10.6 us
    all_to_all x1, starting transfers between devices, on_device(): lax.all_to_all(value, 'space', split_axis=2, concat_axis=1, tiled=True)  8.27 us
    all_to_all x1, waiting for transfers between devices, on_device(): lax.all_to_all(column_out, 'space', split_axis=1, concat_axis=2, tiled=True)  6.45 us
    all_to_all x1, starting transfers between devices, on_device(): lax.all_to_all(maps, 'space', split_axis=2, concat_axis=1, tiled=True)  6.27 us
    all_to_all x1, waiting for transfers between devices, on_device(): lax.all_to_all(value, 'space', split_axis=2, concat_axis=1, tiled=True)  6.2 us
  transfers between devices with their start and end apart: 6, of which 6 were waited for; matrix products, arithmetic and copies ran while one was open for 8% of the time, Pallas kernels for 0%

profile of v1, /device:TPU:19, one launch (start us, length us, event | category | flops | bytes accessed | tf_op | source)
XLA Modules:
  0.0 216.6 jit_solution(8658991779919762531)
XLA Ops:
  6.5 1.9 convert_element_type.86
  8.5 0.7 neg.11
  9.1 43.3 %all-gather.3.cloned.1.call-done = bf16[16,2,128,256]{3,2,1,0:T(8,128)(2,1)} async-done(((bf16[2,2,128,256]{3,2,1,0:T(8,128)(2,1)}), bf16[16,2,128,256]{3,2,1,0:T(8,128)(2,1)}) %all-gather.3.cloned.1.call-update) | async-done | bytes 2097168 | tf_op jit(solution)/shard_map/all_gather | solution.py:52
  52.5 2.2 %fusion = f32[2,2,128]{2,1,0:T(2,128)S(1)} fusion(bf16[8,2,2,128,256]{4,3,2,1,0:T(8,128)(2,1)} %bitcast.85), kind=kLoop, calls=%fused_computation.2 | loop fusion | flops 3145216 | bytes 2099200 | tf_op jit(solution)/shard_map/reduce_sum | solution.py:54
  56.4 1.3 copy-done.1
  57.7 0.7 multiply_convert_fusion.8
  58.4 0.8 copy.56
  59.2 10.9 %all-to-all-start.2 = ((bf16[2,2,128,6]{3,1,0,2:T(2,128)(2,1)}), bf16[2,2,128,6]{3,1,0,2:T(2,128)(2,1)S(1)}, u32[]{:S(2)}, u32[]{:S(2)}) async-start(bf16[2,2,128,6]{3,1,0,2:T(2,128)(2,1)} %copy.56), calls=%async_computation.2 | async-start | bytes 262144 | tf_op jit(solution)/shard_map/all_to_all | solution.py:75
  70.2 2.6 %convolution_convert_fusion.1 = bf16[2,2,128,256]{3,2,1,0:T(8,128)(2,1)S(1)} fusion(bf16[2,2,128,2048]{3,2,1,0:T(8,128)(2,1)} %copy-done.1, bf16[2048,256]{1,0:T(8,128)(2,1)} %param.13), kind=kOutput, calls=%fused_computation.13 | convolution fusion | flops 537001984 | bytes 3407872 | tf_op jit(solution)/shard_map/irwd,dc->irwc/dot_general | solution.py:59
  72.7 1.0 copy.52
  73.7 5.4 %all-to-all-done.2 = bf16[2,2,128,6]{3,1,0,2:T(2,128)(2,1)S(1)} async-done(((bf16[2,2,128,6]{3,1,0,2:T(2,128)(2,1)}), bf16[2,2,128,6]{3,1,0,2:T(2,128)(2,1)S(1)}, u32[]{:S(2)}, u32[]{:S(2)}) %all-to-all-start.2) | async-done | bytes 6176 | tf_op jit(solution)/shard_map/all_to_all | solution.py:75
  79.1 6.3 %all-to-all-start.1 = ((bf16[2,2,128,256]{3,1,0,2:T(2,128)(2,1)}), bf16[2,2,128,256]{3,1,0,2:T(2,128)(2,1)}, u32[]{:S(2)}, u32[]{:S(2)}) async-start(bf16[2,2,128,256]{3,1,0,2:T(2,128)(2,1)} %copy.52), calls=%async_computation.1 | async-start | bytes 524288 | tf_op jit(solution)/shard_map/all_to_all | solution.py:74
  85.5 0.7 mul.108
  86.5 4.2 %multiply_convert_fusion.6 = (bf16[2,2,128,384]{3,2,1,0:T(8,128)(2,1)S(1)}, f32[2,2,128,384]{3,2,1,0:T(8,128)}) fusion(f32[2,2,128,384]{3,2,1,0:T(8,128)S(1)} %copy.48, bf16[2,2,128,2048]{3,2,1,0:T(8,128)(2,1)} %copy-done.1, bf16[2048,384]{1,0:T(8,128)(2,1)} %param.12), kind=kOutput, calls=%fused_computation.33 | convolution fusion | flops 806092800 | bytes 5636096 | tf_op jit(solution)/shard_map/irwd,dc->irwc/dot_general | solution.py:56
  90.7 1.2 copy.50
  91.8 2.8 %all-to-all-done.1 = bf16[2,2,128,256]{3,1,0,2:T(2,128)(2,1)} async-done(((bf16[2,2,128,256]{3,1,0,2:T(2,128)(2,1)}), bf16[2,2,128,256]{3,1,0,2:T(2,128)(2,1)}, u32[]{:S(2)}, u32[]{:S(2)}) %all-to-all-start.1) | async-done | bytes 262176 | tf_op jit(solution)/shard_map/all_to_all | solution.py:74
  94.7 8.3 %all-to-all-start = ((bf16[2,2,128,384]{3,1,0,2:T(2,128)(2,1)}), bf16[2,2,128,384]{3,1,0,2:T(2,128)(2,1)S(1)}, u32[]{:S(2)}, u32[]{:S(2)}) async-start(bf16[2,2,128,384]{3,1,0,2:T(2,128)(2,1)} %copy.50), calls=%async_computation | async-start | bytes 786432 | tf_op jit(solution)/shard_map/all_to_all | solution.py:73
  104.2 1.1 reduce_window_sum.18
  105.3 1.2 copy.53
  106.9 6.2 %all-to-all-done = bf16[2,2,128,384]{3,1,0,2:T(2,128)(2,1)S(1)} async-done(((bf16[2,2,128,384]{3,1,0,2:T(2,128)(2,1)}), bf16[2,2,128,384]{3,1,0,2:T(2,128)(2,1)S(1)}, u32[]{:S(2)}, u32[]{:S(2)}) %all-to-all-start) | async-done | bytes 393248 | tf_op jit(solution)/shard_map/all_to_all | solution.py:73
  113.4 1.6 reshape.71
  115.0 2.5 %convolution_convert_fusion = bf16[2,2,6,64,128]{4,3,2,1,0:T(8,128)(2,1)S(1)} fusion(bf16[2,128,2,6,64]{4,3,2,1,0:T(8,128)(2,1)} %reshape.71, f32[2,2,6,128]{3,2,1,0:T(8,128)S(1)} %bitcast_subtract_fusion, f32[2,2,6,128]{3,2,1,0:T(8,128)S(1)} %reduce_window_sum.18, f32[2,2,128,128]{3,2,1,0:T(8,128)S(1)} %fusion.35, pred[128,128]{1,0:T(8,128)(4,1)S(1)} %copy-done.5, ...), kind=kOutput, calls=%fused_computation.12 | convolution fusion | flops 53280768 | bytes 1105920 | tf_op jit(solution)/shard_map/iahlm,imahp->ilahp/dot_general | solution.py:43
  117.5 1.1 copy.62
  118.6 10.6 %all-to-all-start.3 = ((bf16[2,128,2,384]{3,2,0,1:T(2,128)(2,1)}), bf16[2,128,2,384]{3,2,0,1:T(2,128)(2,1)S(1)}, u32[]{:S(2)}, u32[]{:S(2)}) async-start(bf16[2,128,2,384]{3,2,0,1:T(2,128)(2,1)} %copy.62), calls=%async_computation.3 | async-start | bytes 786432 | tf_op jit(solution)/shard_map/all_to_all | solution.py:77
  129.5 1.2 reduce_window_sum.17
  131.0 1.8 fusion.12
  133.0 6.4 %all-to-all-done.3 = bf16[2,128,2,384]{3,2,0,1:T(2,128)(2,1)S(1)} async-done(((bf16[2,128,2,384]{3,2,0,1:T(2,128)(2,1)}), bf16[2,128,2,384]{3,2,0,1:T(2,128)(2,1)S(1)}, u32[]{:S(2)}, u32[]{:S(2)}) %all-to-all-start.3) | async-done | bytes 393248 | tf_op jit(solution)/shard_map/all_to_all | solution.py:77
  140.4 1.4 reshape.73
  141.9 1.6 multiply_reduce_fusion
  143.5 3.3 %fusion.1 = f32[2,2,128,2048]{3,2,1,0:T(8,128)} fusion(bf16[384,2048]{1,0:T(8,128)(2,1)S(1)} %copy-done, f32[2,2,128,384]{3,2,1,0:T(8,128)S(1)} %get-tuple-element.6, f32[384]{0:T(512)S(1)} %copy-done.11, f32[2,2,128]{2,1,0:T(2,128)S(1)} %add_rsqrt_fusion), kind=kOutput, calls=%fused_computation.4 | convolution fusion | flops 805896192 | bytes 6557184 | tf_op jit(solution)/shard_map/irwc,cd->irwd/dot_general | solution.py:85
  146.8 61.2 %reduce-scatter.2.cloned.1.call-done = f32[2,2,128,256]{3,2,1,0:T(8,128)} async-done(((f32[2,2,128,2048]{3,2,1,0:T(8,128)}), f32[2,2,128,256]{3,2,1,0:T(8,128)}) %reduce-scatter.2.cloned.1.call-update) | async-done | bytes 524304 | tf_op jit(solution)/shard_map/reduce_scatter | solution.py:86
  208.0 1.8 add_convert_fusion
  (56 shorter events, 5.8 us)
Async XLA Ops:
  6.5 136.9 %copy-start = (bf16[384,2048]{1,0:T(8,128)(2,1)S(1)}, bf16[384,2048]{1,0:T(8,128)(2,1)}, u32[]{:S(2)}) copy-start(bf16[384,2048]{1,0:T(8,128)(2,1)} %param.19) | copy-start | bytes 4718596
  6.5 45.9 %all-gather.3.cloned.1.call-start = ((), (), s32[]{:S(2)}) async-start(), calls=%async_computation.6 | async-start | bytes 2359296 | tf_op jit(solution)/shard_map/all_gather | solution.py:52
  9.1 47.3 %copy-start.7 = (f32[6]{0:T(128)}, f32[6]{0:T(128)S(1)}, u32[]{:S(2)}) copy-start(f32[6]{0:T(128)S(1)} %neg.11) | copy-start | bytes 76
  52.5 2.2 %copy-start.2 = (bf16[16,2,128,256]{3,2,1,0:T(8,128)(2,1)S(1)}, bf16[16,2,128,256]{3,2,1,0:T(8,128)(2,1)}, u32[]{:S(2)}) copy-start(bf16[16,2,128,256]{3,2,1,0:T(8,128)(2,1)} %all-gather.3.cloned.1.call-done) | copy-start | bytes 6291460
  55.2 0.7 copy-start.9
  55.9 1.8 copy-start.4
  55.9 1.8 copy-start.12
  56.4 1.3 copy-start.1
  59.2 19.9 %all-to-all-start.2 = ((bf16[2,2,128,6]{3,1,0,2:T(2,128)(2,1)}), bf16[2,2,128,6]{3,1,0,2:T(2,128)(2,1)S(1)}, u32[]{:S(2)}, u32[]{:S(2)}) async-start(bf16[2,2,128,6]{3,1,0,2:T(2,128)(2,1)} %copy.56), calls=%async_computation.2 | async-start | bytes 262144 | tf_op jit(solution)/shard_map/all_to_all | solution.py:75
  70.1 15.3 %copy-start.13 = (f32[6]{0:T(128)S(1)}, f32[6]{0:T(128)}, u32[]{:S(2)}) copy-start(f32[6]{0:T(128)} %param.17) | copy-start | bytes 76
  79.1 15.5 %all-to-all-start.1 = ((bf16[2,2,128,256]{3,1,0,2:T(2,128)(2,1)}), bf16[2,2,128,256]{3,1,0,2:T(2,128)(2,1)}, u32[]{:S(2)}, u32[]{:S(2)}) async-start(bf16[2,2,128,256]{3,1,0,2:T(2,128)(2,1)} %copy.52), calls=%async_computation.1 | async-start | bytes 524288 | tf_op jit(solution)/shard_map/all_to_all | solution.py:74
  94.7 18.4 %all-to-all-start = ((bf16[2,2,128,384]{3,1,0,2:T(2,128)(2,1)}), bf16[2,2,128,384]{3,1,0,2:T(2,128)(2,1)S(1)}, u32[]{:S(2)}, u32[]{:S(2)}) async-start(bf16[2,2,128,384]{3,1,0,2:T(2,128)(2,1)} %copy.50), calls=%async_computation | async-start | bytes 786432 | tf_op jit(solution)/shard_map/all_to_all | solution.py:73
  106.5 8.5 %copy-start.5 = (pred[128,128]{1,0:T(8,128)(4,1)S(1)}, pred[128,128]{1,0:T(8,128)(4,1)}, u32[]{:S(2)}) copy-start(pred[128,128]{1,0:T(8,128)(4,1)} %get-tuple-element.14) | copy-start | bytes 49156
  106.5 8.5 %copy-start.6 = (pred[128,128]{1,0:T(8,128)(4,1)S(1)}, pred[128,128]{1,0:T(8,128)(4,1)}, u32[]{:S(2)}) copy-start(pred[128,128]{1,0:T(8,128)(4,1)} %get-tuple-element.15) | copy-start | bytes 49156
  117.5 11.7 %copy-start.8 = (f32[6]{0:T(128)S(1)}, f32[6]{0:T(128)}, u32[]{:S(2)}) copy-start(f32[6]{0:T(128)} %copy-done.7) | copy-start | bytes 76
  118.6 20.9 %all-to-all-start.3 = ((bf16[2,128,2,384]{3,2,0,1:T(2,128)(2,1)}), bf16[2,128,2,384]{3,2,0,1:T(2,128)(2,1)S(1)}, u32[]{:S(2)}, u32[]{:S(2)}) async-start(bf16[2,128,2,384]{3,2,0,1:T(2,128)(2,1)} %copy.62), calls=%async_computation.3 | async-start | bytes 786432 | tf_op jit(solution)/shard_map/all_to_all | solution.py:77
  129.2 78.8 %reduce-scatter.2.cloned.1.call-start = ((), (), s32[]{:S(2)}) async-start(), calls=%async_computation.5 | async-start | bytes 4718592 | tf_op jit(solution)/shard_map/reduce_scatter | solution.py:86
  140.2 1.7 copy-start.10
  141.9 1.6 copy-start.11
  146.8 61.2 %copy-start.3 = (f32[2,2,128,256]{3,2,1,0:T(8,128)S(1)}, f32[2,2,128,256]{3,2,1,0:T(8,128)}, u32[]{:S(2)}) copy-start(f32[2,2,128,256]{3,2,1,0:T(8,128)} %param.10) | copy-start | bytes 1572868
Sparse Core Ops, SparseCore 0:
  9.5 42.9 all-gather.2
  146.9 61.0 reduce-scatter.1
